TPU v7x, 32 devices: a whole 2x2x4 slice. The times are simulated.
32 devices in a mesh: fsdp: 4 (over y, x), tenant: 4 (over z), dp: 2 (over core).
Axes of the slice: x: 2, y: 2, z: 4, core: 2. Of those that a mesh axis runs over, the one named last changes fastest.
Arguments:
- tokens: bfloat16 [3072, 5120], P(('fsdp', 'dp'), 'tenant'), may hold values from -6 to 6
- block_tenant_index: int32 [48], P(('fsdp', 'dp')), may hold values from 0 to 7
- ranks: int32 [8], replicated, may hold values from 16 to 64, as said below
- frozen_up_weight: bfloat16 [5120, 14336], P(('fsdp', 'dp'), 'tenant'), may hold values from -0.078125 to 0.078125
- tenant_down_adapters: bfloat16 [8, 64, 5120], P('tenant'), may hold values from -0.078125 to 0.078125
- tenant_up_adapters: bfloat16 [8, 64, 14336], P('tenant'), may hold values from -0.75 to 0.75
- cotangent: bfloat16 [3072, 14336], P(('fsdp', 'dp'), 'tenant'), may hold values from -6 to 6
Outputs:
- hidden_out: bfloat16 [3072, 14336], P(('fsdp', 'dp'), 'tenant')
- grad_tokens: bfloat16 [3072, 5120], P(('fsdp', 'dp'), 'tenant')
- grad_down: float32 [8, 64, 5120], P('dp', None, 'tenant')
- grad_up: float32 [8, 64, 14336], P('dp', None, 'tenant')
Inputs may be any that keep to these rules, and one draw needn't show every extreme that they name: `ranks`: multiples of 16; some tenant has rank 64.
All inputs are finite; a program needn't handle non-finite values.
Results may differ from a plain program's by a relative error of at most 0.0034.
Values may be sent and summed in bfloat16 or wider, within the bound.
No kernel may reach another device: no remote copies, remote signals or barrier semaphores. Data moves between devices by JAX's collectives and lax.ppermute only.
A program may use at most 128 MiB of HBM per device.

v0:
```python
import jax
import jax.numpy as jnp
from jax import lax
from jax.sharding import PartitionSpec as P

BLOCK = 64
alpha_scale = 32.0


def make_gain(block_tenant_index, ranks, rows, largest_rank):
    tenants = ranks.shape[0]
    rows_tenant = jnp.repeat(block_tenant_index, BLOCK, total_repeat_length=rows)
    columns = jnp.arange(tenants * largest_rank, dtype=jnp.int32)
    col_tenant = columns // largest_rank
    col_slot = columns % largest_rank
    ranks_col = jnp.repeat(ranks, largest_rank, total_repeat_length=tenants * largest_rank)
    keep = (rows_tenant[:, None] == col_tenant[None, :]) & (col_slot[None, :] < ranks_col[None, :])
    scale_col = alpha_scale / ranks_col.astype(jnp.float32)
    return jnp.where(keep, scale_col[None, :], jnp.float32(0.0))


def shards(
    tokens,
    block_tenant_index,
    ranks,
    frozen_up_weight,
    tenant_down_adapters,
    tenant_up_adapters,
    cotangent,
):
    rows = tokens.shape[0]
    local_d = tokens.shape[1]
    local_f = cotangent.shape[1]
    tenants = ranks.shape[0]
    largest_rank = tenant_down_adapters.shape[1]
    gain = make_gain(block_tenant_index, ranks, rows, largest_rank)
    whole = lax.all_gather(tokens, "tenant", axis=1, tiled=True)
    weight = lax.all_gather(frozen_up_weight, ("fsdp", "dp"), axis=0, tiled=True)
    down_part, up_adapter_slice = (
        lax.all_to_all(tenant_down_adapters, "tenant", split_axis=2, concat_axis=0, tiled=True),
        lax.all_to_all(tenant_up_adapters, "tenant", split_axis=2, concat_axis=0, tiled=True),
    )
    local_down = down_part.reshape(tenants * largest_rank, local_d)
    partial_proj = lax.dot_general(
        tokens, local_down, (((1,), (1,)), ((), ())), preferred_element_type=jnp.float32
    )
    proj = lax.psum(partial_proj, "tenant")
    flattened_up = up_adapter_slice.reshape(tenants * largest_rank, local_f)
    adapted = (proj * gain).astype(jnp.bfloat16)
    base = jnp.dot(whole, weight, preferred_element_type=jnp.float32)
    hidden_out = (base + jnp.dot(adapted, flattened_up, preferred_element_type=jnp.float32)).astype(
        jnp.bfloat16
    )
    back_part = lax.dot_general(
        cotangent, flattened_up, (((1,), (1,)), ((), ())), preferred_element_type=jnp.float32
    )
    back = lax.psum(back_part, "tenant")
    adapted_grad = (back * gain).astype(jnp.bfloat16)
    base_back = lax.dot_general(
        cotangent, weight, (((1,), (1,)), ((), ())), preferred_element_type=jnp.float32
    )
    grad_base = lax.psum_scatter(base_back, "tenant", scatter_dimension=1, tiled=True)
    grad_tokens = (
        grad_base + jnp.dot(adapted_grad, local_down, preferred_element_type=jnp.float32)
    ).astype(jnp.bfloat16)
    up_term = lax.dot_general(
        adapted, cotangent, (((0,), (0,)), ((), ())), preferred_element_type=jnp.float32
    )
    down_term = lax.dot_general(
        adapted_grad, tokens, (((0,), (0,)), ((), ())), preferred_element_type=jnp.float32
    )
    up_term = up_term.reshape(tenants, largest_rank, local_f)
    down_term = down_term.reshape(tenants, largest_rank, local_d)
    down_share, up_share = (
        lax.psum_scatter(down_term, "dp", scatter_dimension=0, tiled=True),
        lax.psum_scatter(up_term, "dp", scatter_dimension=0, tiled=True),
    )
    grad_down, grad_up = lax.psum((down_share, up_share), "fsdp")
    return (hidden_out, grad_tokens, grad_down, grad_up)


def solution(mesh):
    return jax.shard_map(
        shards,
        mesh=mesh,
        in_specs=(
            P(("fsdp", "dp"), "tenant"),
            P(("fsdp", "dp")),
            P(),
            P(("fsdp", "dp"), "tenant"),
            P("tenant", None, None),
            P("tenant", None, None),
            P(("fsdp", "dp"), "tenant"),
        ),
        out_specs=(
            P(("fsdp", "dp"), "tenant"),
            P(("fsdp", "dp"), "tenant"),
            P("dp", None, "tenant"),
            P("dp", None, "tenant"),
        ),
        check_vma=False,
    )
```

profile of v0, /device:TPU:0, one launch (start us, length us, event | category | flops | bytes accessed | tf_op | source)
XLA Modules:
  0.0 692.7 jit_solution(15375952981959615952)
XLA Ops:
  8.0 6.4 copy.13
  14.5 4.7 reshape.322
  19.1 6.3 all-to-all-start
  25.5 15.8 %copy.16 = bf16[2,64,14336]{1,0,2:T(2,128)(2,1)} copy(bf16[2,64,14336]{2,1,0:T(8,128)(2,1)} %param.16) | data formatting | bytes 7340032 | tf_op args[5]
  41.3 8.6 %reshape.320 = bf16[4,2,229376]{2,1,0:T(2,128)(2,1)} reshape(bf16[14336,2,64]{2,1,0:T(2,128)(2,1)} %bitcast.77) | data formatting | bytes 7340032
  49.9 7.1 %all-to-all-done = bf16[4,2,81920]{2,1,0:T(2,128)(2,1)} async-done(((bf16[4,2,81920]{2,1,0:T(2,128)(2,1)}), bf16[4,2,81920]{2,1,0:T(2,128)(2,1)}, u32[]{:S(2)}, u32[]{:S(2)}) %all-to-all-start) | async-done | bytes 1310752 | tf_op jit(solution)/shard_map/all_to_all | solution.py:40
  56.9 4.8 all-to-all-start.1
  61.8 4.6 reshape.323
  66.4 7.4 %copy.19 = bf16[2,64,4,1280]{3,2,1,0:T(4,128)(2,1)} copy(bf16[2,64,4,1280]{1,0,3,2:T(2,128)(2,1)} %bitcast.82) | data formatting | bytes 2621440 | tf_op jit(solution)/shard_map/all_to_all | solution.py:40
  79.1 64.2 %all-to-all-done.1 = bf16[4,2,229376]{2,1,0:T(2,128)(2,1)} async-done(((bf16[4,2,229376]{2,1,0:T(2,128)(2,1)}), bf16[4,2,229376]{2,1,0:T(2,128)(2,1)}, u32[]{:S(2)}, u32[]{:S(2)}) %all-to-all-start.1) | async-done | bytes 3670048 | tf_op jit(solution)/shard_map/all_to_all | solution.py:41
  143.3 8.4 %reshape.321 = bf16[14336,2,64]{2,1,0:T(2,128)(2,1)} reshape(bf16[4,2,229376]{2,1,0:T(2,128)(2,1)} %all-to-all-done.1) | data formatting | bytes 7340032
  151.7 18.7 %copy.20 = bf16[2,64,4,3584]{3,2,1,0:T(4,128)(2,1)} copy(bf16[2,64,4,3584]{1,0,3,2:T(2,128)(2,1)} %bitcast.76) | data formatting | bytes 7340032 | tf_op jit(solution)/shard_map/all_to_all | solution.py:41
  183.5 4.5 compare_select_fusion.2
  188.9 56.8 %all-reduce.5.cloned.1.call-done = (f32[384,512]{1,0:T(8,128)}, f32[384,512]{1,0:T(8,128)}) async-done(((f32[384,512]{1,0:T(8,128)}, f32[384,512]{1,0:T(8,128)}), (f32[384,512]{1,0:T(8,128)}, f32[384,512]{1,0:T(8,128)})) %all-reduce.5.cloned.1.call-update) | async-done | bytes 1572880 | tf_op jit(solution)/shard_map/psum | solution.py:47
  245.7 4.0 fusion.17
  249.8 7.1 %fusion.20 = f32[512,3584]{1,0:T(8,128)} fusion(bf16[384,3584]{1,0:T(8,128)(2,1)S(1)} %copy-done, f32[384,512]{1,0:T(8,128)S(1)} %copy-done.5, f32[512]{0:T(512)S(1)} %convert_divide_fusion, s32[512]{0:T(512)S(1)} %add_select_fusion, s32[384]{0:T(512)S(1)} %and_select_fusion, pred[512]{0:T(512)(128)(4,1)S(1)} %get-tuple-element.32), kind=kOutput, calls=%fused_computation.52 | convolution fusion | flops 1410269184 | bytes 10885120 | tf_op jit(solution)/shard_map/dot_general | solution.py:66
  257.7 96.2 %all-gather.5.cloned.1.call-done = bf16[5120,3584]{1,0:T(8,128)(2,1)} async-done(((bf16[640,3584]{1,0:T(8,128)(2,1)}), bf16[5120,3584]{1,0:T(8,128)(2,1)}) %all-gather.5.cloned.1.call-update) | async-done | bytes 36700176 | tf_op jit(solution)/shard_map/all_gather | solution.py:38
  353.9 22.1 %fusion.27 = f32[384,5120]{1,0:T(8,128)} fusion(bf16[384,3584]{1,0:T(8,128)(2,1)S(1)} %copy-done, bf16[5120,3584]{1,0:T(8,128)(2,1)} %all-gather.5.cloned.1.call-done), kind=kOutput, calls=%fused_computation.57 | convolution fusion | flops 14092861440 | bytes 47316992 | tf_op jit(solution)/shard_map/dot_general | solution.py:59
  376.6 139.9 %all-gather.3.cloned.1.call-done = bf16[384,5120]{1,0:T(8,128)(2,1)} async-done(((bf16[384,1280]{1,0:T(8,128)(2,1)}), bf16[384,5120]{1,0:T(8,128)(2,1)}) %all-gather.3.cloned.1.call-update) | async-done | bytes 3932176 | tf_op jit(solution)/shard_map/all_gather | solution.py:37
  516.5 23.5 %fusion.25 = f32[384,3584]{1,0:T(8,128)} fusion(bf16[384,5120]{1,0:T(8,128)(2,1)} %all-gather.3.cloned.1.call-done, bf16[5120,3584]{1,0:T(8,128)(2,1)} %all-gather.5.cloned.1.call-done), kind=kOutput, calls=%fused_computation.55 | convolution fusion | flops 14092861440 | bytes 46137344 | tf_op jit(solution)/shard_map/dot_general | solution.py:50
  540.0 7.0 %fusion = bf16[384,3584]{1,0:T(8,128)(2,1)} fusion(f32[384,3584]{1,0:T(8,128)} %fusion.25, bf16[512,3584]{1,0:T(8,128)(2,1)} %bitcast.79, f32[384,512]{1,0:T(8,128)S(1)} %copy-done.5, f32[512]{0:T(512)S(1)} %convert_divide_fusion, s32[512]{0:T(512)S(1)} %add_select_fusion, s32[384]{0:T(512)S(1)} %and_select_fusion, pred[512]{0:T(512)(128)(4,1)S(1)} %get-tuple-element.32), kind=kOutput, calls=%fused_computation.1 | convolution fusion | flops 1413021696 | bytes 12720128 | tf_op jit(solution)/shard_map/dot_general | solution.py:51
  547.0 10.7 %reduce-scatter.4.cloned.1.call-done = f32[384,1280]{1,0:T(8,128)} async-done(((f32[384,5120]{1,0:T(8,128)}), f32[384,1280]{1,0:T(8,128)}) %reduce-scatter.4.cloned.1.call-update) | async-done | bytes 1966096 | tf_op jit(solution)/shard_map/reduce_scatter | solution.py:62
  561.0 117.8 %all-reduce.7.cloned.1.call-done = (f32[4,64,1280]{2,1,0:T(8,128)}, f32[4,64,3584]{2,1,0:T(8,128)}) async-done(((f32[4,64,1280]{2,1,0:T(8,128)}, f32[4,64,3584]{2,1,0:T(8,128)}), (f32[4,64,1280]{2,1,0:T(8,128)}, f32[4,64,3584]{2,1,0:T(8,128)})) %all-reduce.7.cloned.1.call-update) | async-done | bytes 4980752 | tf_op jit(solution)/shard_map/psum | solution.py:78
  681.4 4.1 copy.30
  (56 shorter events, 26.6 us)
Async XLA Ops:
  8.0 166.9 %copy-start = (bf16[384,3584]{1,0:T(8,128)(2,1)S(1)}, bf16[384,3584]{1,0:T(8,128)(2,1)}, u32[]{:S(2)}) copy-start(bf16[384,3584]{1,0:T(8,128)(2,1)} %param.17) | copy-start | bytes 8257540
  19.1 37.8 %all-to-all-start = ((bf16[4,2,81920]{2,1,0:T(2,128)(2,1)}), bf16[4,2,81920]{2,1,0:T(2,128)(2,1)}, u32[]{:S(2)}, u32[]{:S(2)}) async-start(bf16[4,2,81920]{2,1,0:T(2,128)(2,1)} %reshape.322), calls=%async_computation | async-start | bytes 2621440 | tf_op jit(solution)/shard_map/all_to_all | solution.py:40
  56.9 86.3 %all-to-all-start.1 = ((bf16[4,2,229376]{2,1,0:T(2,128)(2,1)}), bf16[4,2,229376]{2,1,0:T(2,128)(2,1)}, u32[]{:S(2)}, u32[]{:S(2)}) async-start(bf16[4,2,229376]{2,1,0:T(2,128)(2,1)} %reshape.320), calls=%async_computation.1 | async-start | bytes 7340032 | tf_op jit(solution)/shard_map/all_to_all | solution.py:41
  61.8 184.0 %all-reduce.5.cloned.1.call-start = ((), (), s32[]{:S(2)}) async-start(), calls=%async_computation.10 | async-start | bytes 3145728 | tf_op jit(solution)/shard_map/psum | solution.py:47
  75.3 1.1 copy-start.3
  173.1 1.8 copy-start.2
  177.4 0.7 copy-start.8
  177.4 1.4 copy-start.7
  177.4 2.1 copy-start.10
  177.4 2.2 copy-start.9
  177.5 176.5 %all-gather.5.cloned.1.call-start = ((), (), s32[]{:S(2)}) async-start(), calls=%async_computation.6 | async-start | bytes 41287680 | tf_op jit(solution)/shard_map/all_gather | solution.py:38
  178.0 198.0 %reduce-scatter.6.cloned.1.call-start = ((), (), s32[]{:S(2)}) async-start(), calls=%async_computation.8 | async-start | bytes 3932160 | tf_op jit(solution)/shard_map/reduce_scatter | solution.py:75
  245.7 4.1 copy-start.5
  249.7 126.4 %reduce-scatter.8.cloned.1.call-start = ((), (), s32[]{:S(2)}) async-start(), calls=%async_computation.9 | async-start | bytes 11010048 | tf_op jit(solution)/shard_map/reduce_scatter | solution.py:76
  256.9 259.6 %all-gather.3.cloned.1.call-start = ((), (), s32[]{:S(2)}) async-start(), calls=%async_computation.5 | async-start | bytes 4915200 | tf_op jit(solution)/shard_map/all_gather | solution.py:37
  257.5 300.2 %reduce-scatter.4.cloned.1.call-start = ((), (), s32[]{:S(2)}) async-start(), calls=%async_computation.7 | async-start | bytes 9830400 | tf_op jit(solution)/shard_map/reduce_scatter | solution.py:62
  376.0 302.8 %all-reduce.7.cloned.1.call-start = ((), (), s32[]{:S(2)}) async-start(), calls=%async_computation.11 | async-start | bytes 9961472 | tf_op jit(solution)/shard_map/psum | solution.py:78
  540.0 17.8 %copy-start.4 = (bf16[4,2,64,1280]{3,2,1,0:T(8,128)(2,1)S(1)}, bf16[4,2,64,1280]{3,2,1,0:T(8,128)(2,1)}, u32[]{:S(2)}) copy-start(bf16[4,2,64,1280]{3,2,1,0:T(8,128)(2,1)} %copy-done.3) | copy-start | bytes 3932164
  540.0 17.8 %copy-start.6 = (f32[384,512]{1,0:T(8,128)S(1)}, f32[384,512]{1,0:T(8,128)}, u32[]{:S(2)}) copy-start(f32[384,512]{1,0:T(8,128)} %get-tuple-element.29) | copy-start | bytes 2359300
  678.8 6.8 copy-start.1
Sparse Core Ops, SparseCore 0:
  177.6 68.0 all-reduce.4
  249.9 16.8 reduce-scatter.5
  269.1 17.2 reduce-scatter.7
  376.1 181.5 reduce-scatter.3
  561.2 117.5 all-reduce.6
Sparse Core Ops, SparseCore 1:
  179.9 174.0 all-gather.4
  355.4 161.1 all-gather.2
where the time goes:
time: 695 us; the launch traced here: 693 us
  waiting for transfers between devices  494 us (71%)
  local copies, waits for them, and re-layouts  89.8 us (13%)
  matrix products  72.2 us (10%)
  between operations  15.4 us (2%)
  starting transfers between devices  11.6 us (2%)
  other arithmetic  9.35 us (1%)
    all_gather x1, waiting for transfers between devices, shards(): whole = lax.all_gather(tokens, 'tenant', axis=1, tiled=True)  140 us
    psum x1, waiting for transfers between devices, shards(): grad_down, grad_up = lax.psum((down_share, up_share), 'fsdp')  118 us
    all_gather x1, waiting for transfers between devices, shards(): lax.all_gather(frozen_up_weight, ('fsdp', 'dp'), axis=0, tiled=True)  96.2 us
    all_to_all x1, waiting for transfers between devices, shards(): lax.all_to_all(tenant_up_adapters, 'tenant', split_axis=2, concat_axis=0,...  64.2 us
    unnamed x30, local copies, waits for them, and re-layouts  58.2 us
    psum x1, waiting for transfers between devices, shards(): proj = lax.psum(partial_proj, 'tenant')  56.8 us
    dot_general x1, matrix products, shards(): base = jnp.dot(whole, weight, preferred_element_type=jnp.float32)  23.5 us
    dot_general x1, matrix products, shards(): lax.dot_general(cotangent, weight, (((1,), (1,)), ((), ())), preferred_el...  22.1 us
  transfers between devices with their start and end apart: 9, of which 7 were waited for; matrix products, arithmetic and copies ran while one was open for 17% of the time, Pallas kernels for 0%

commit v1 on v0

--- a/solution.py
+++ b/solution.py
@@ -44,7 +44,8 @@
     partial_proj = lax.dot_general(
         tokens, local_down, (((1,), (1,)), ((), ())), preferred_element_type=jnp.float32
     )
-    proj = lax.psum(partial_proj, "tenant")
+    shards_2 = lax.all_gather(partial_proj, "tenant")
+    proj = jnp.sum(shards_2, axis=0)
     flattened_up = up_adapter_slice.reshape(tenants * largest_rank, local_f)
     adapted = (proj * gain).astype(jnp.bfloat16)
     base = jnp.dot(whole, weight, preferred_element_type=jnp.float32)

time: 695 us -> 830 us (1.19)
  waiting for transfers between devices: 494 us -> 630 us
    reduce_scatter x1, waiting for transfers between devices: 10.7 us -> 106 us  [shards(): lax.psum_scatter(base_back, 'tenant', scatter_dimension=1, tiled=True)]
    all_gather x1, waiting for transfers between devices: 96.2 us -> 167 us  [shards(): lax.all_gather(frozen_up_weight, ('fsdp', 'dp'), axis=0, tiled=True)]
    all_gather x0 -> x1, waiting for transfers between devices: none -> 60.9 us  [shards(): shards_2 = lax.all_gather(partial_proj, 'tenant')]
    all_gather x1, waiting for transfers between devices: 140 us -> 79.1 us  [shards(): whole = lax.all_gather(tokens, 'tenant', axis=1, tiled=True)]
    psum x1, waiting for transfers between devices: 56.8 us -> 16.3 us  [shards(): back = lax.psum(back_part, 'tenant')]
    reduce_scatter x1, waiting for transfers between devices: 0.02 us -> 10.6 us  [shards(): lax.psum_scatter(up_term, 'dp', scatter_dimension=0, tiled=True)]
    unnamed x30 -> x28, local copies, waits for them, and re-layouts: 58.2 us -> 58.3 us
  transfers between devices with their start and end apart: 9 -> 10, of which waited for: 7 -> 8; matrix products, arithmetic and copies ran while one was open for 17% -> 17% of each run, Pallas kernels for 0% -> 0%
where the time goes in v1:
time: 830 us; the launch traced here: 828 us
  waiting for transfers between devices  630 us (76%)
  local copies, waits for them, and re-layouts  89.9 us (11%)
  matrix products  71.1 us (9%)
  between operations  14.3 us (2%)
  other arithmetic  11.7 us (1%)
  starting transfers between devices  11.1 us (1%)
    all_gather x1, waiting for transfers between devices, shards(): lax.all_gather(frozen_up_weight, ('fsdp', 'dp'), axis=0, tiled=True)  167 us
    psum x1, waiting for transfers between devices, shards(): grad_down, grad_up = lax.psum((down_share, up_share), 'fsdp')  117 us
    reduce_scatter x1, waiting for transfers between devices, shards(): lax.psum_scatter(base_back, 'tenant', scatter_dimension=1, tiled=True)  106 us
    all_gather x1, waiting for transfers between devices, shards(): whole = lax.all_gather(tokens, 'tenant', axis=1, tiled=True)  79.1 us
    all_to_all x1, waiting for transfers between devices, shards(): lax.all_to_all(tenant_up_adapters, 'tenant', split_axis=2, concat_axis=0,...  71.1 us
    all_gather x1, waiting for transfers between devices, shards(): shards_2 = lax.all_gather(partial_proj, 'tenant')  60.9 us
    unnamed x28, local copies, waits for them, and re-layouts  58.3 us
    dot_general x1, matrix products, shards(): base = jnp.dot(whole, weight, preferred_element_type=jnp.float32)  23.9 us
  transfers between devices with their start and end apart: 10, of which 8 were waited for; matrix products, arithmetic and copies ran while one was open for 17% of the time, Pallas kernels for 0%

profile of v1, /device:TPU:0, one launch (start us, length us, event | category | flops | bytes accessed | tf_op | source)
XLA Modules:
  0.0 827.9 jit_solution(12817699277916810195)
XLA Ops:
  7.2 15.9 %copy.16 = bf16[2,64,14336]{1,0,2:T(2,128)(2,1)} copy(bf16[2,64,14336]{2,1,0:T(8,128)(2,1)} %param.16) | data formatting | bytes 7340032 | tf_op args[5]
  23.1 8.6 %reshape.321 = bf16[4,2,229376]{2,1,0:T(2,128)(2,1)} reshape(bf16[14336,2,64]{2,1,0:T(2,128)(2,1)} %bitcast.78) | data formatting | bytes 7340032
  31.7 6.3 all-to-all-start.1
  38.1 6.3 copy.13
  44.4 4.7 reshape.323
  49.0 71.1 %all-to-all-done.1 = bf16[4,2,229376]{2,1,0:T(2,128)(2,1)} async-done(((bf16[4,2,229376]{2,1,0:T(2,128)(2,1)}), bf16[4,2,229376]{2,1,0:T(2,128)(2,1)}, u32[]{:S(2)}, u32[]{:S(2)}) %all-to-all-start.1) | async-done | bytes 3670048 | tf_op jit(solution)/shard_map/all_to_all | solution.py:41
  120.2 4.3 all-to-all-start
  124.5 8.4 %reshape.322 = bf16[14336,2,64]{2,1,0:T(2,128)(2,1)} reshape(bf16[4,2,229376]{2,1,0:T(2,128)(2,1)} %all-to-all-done.1) | data formatting | bytes 7340032
  133.0 18.7 %copy.20 = bf16[2,64,4,3584]{3,2,1,0:T(4,128)(2,1)} copy(bf16[2,64,4,3584]{1,0,3,2:T(2,128)(2,1)} %bitcast.77) | data formatting | bytes 7340032 | tf_op jit(solution)/shard_map/all_to_all | solution.py:41
  158.8 4.6 reshape.324
  163.4 7.4 copy.19
  182.6 4.4 compare_select_fusion.2
  187.8 16.3 %all-reduce.4.cloned.1.call-done = f32[384,512]{1,0:T(8,128)} async-done(((f32[384,512]{1,0:T(8,128)}), f32[384,512]{1,0:T(8,128)}) %all-reduce.4.cloned.1.call-update) | async-done | bytes 786448 | tf_op jit(solution)/shard_map/psum | solution.py:58
  208.0 60.9 %all-gather.9.cloned.1.call-done = f32[1536,512]{1,0:T(8,128)} async-done(((f32[384,512]{1,0:T(8,128)}), f32[1536,512]{1,0:T(8,128)}) %all-gather.9.cloned.1.call-update) | async-done | bytes 3145744 | tf_op jit(solution)/shard_map/all_gather | solution.py:47
  271.2 5.4 fusion.20
  277.5 167.1 %all-gather.7.cloned.1.call-done = bf16[5120,3584]{1,0:T(8,128)(2,1)} async-done(((bf16[640,3584]{1,0:T(8,128)(2,1)}), bf16[5120,3584]{1,0:T(8,128)(2,1)}) %all-gather.7.cloned.1.call-update) | async-done | bytes 36700176 | tf_op jit(solution)/shard_map/all_gather | solution.py:38
  444.6 22.1 %fusion.27 = f32[384,5120]{1,0:T(8,128)} fusion(bf16[384,3584]{1,0:T(8,128)(2,1)S(1)} %copy-done, bf16[5120,3584]{1,0:T(8,128)(2,1)} %all-gather.7.cloned.1.call-done), kind=kOutput, calls=%fused_computation.57 | convolution fusion | flops 14092861440 | bytes 47316992 | tf_op jit(solution)/shard_map/dot_general | solution.py:60
  466.8 10.6 %reduce-scatter.8.cloned.1.call-done = f32[4,64,3584]{2,1,0:T(8,128)} async-done(((f32[8,64,3584]{2,1,0:T(8,128)}), f32[4,64,3584]{2,1,0:T(8,128)}) %reduce-scatter.8.cloned.1.call-update) | async-done | bytes 3670032 | tf_op jit(solution)/shard_map/reduce_scatter | solution.py:77
  477.4 79.1 %all-gather.5.cloned.1.call-done = bf16[384,5120]{1,0:T(8,128)(2,1)} async-done(((bf16[384,1280]{1,0:T(8,128)(2,1)}), bf16[384,5120]{1,0:T(8,128)(2,1)}) %all-gather.5.cloned.1.call-update) | async-done | bytes 3932176 | tf_op jit(solution)/shard_map/all_gather | solution.py:37
  556.5 23.9 %fusion.25 = f32[384,3584]{1,0:T(8,128)} fusion(bf16[384,5120]{1,0:T(8,128)(2,1)} %all-gather.5.cloned.1.call-done, bf16[5120,3584]{1,0:T(8,128)(2,1)} %all-gather.7.cloned.1.call-done), kind=kOutput, calls=%fused_computation.55 | convolution fusion | flops 14092861440 | bytes 46137344 | tf_op jit(solution)/shard_map/dot_general | solution.py:51
  580.4 7.0 fusion
  587.5 106.2 %reduce-scatter.4.cloned.1.call-done = f32[384,1280]{1,0:T(8,128)} async-done(((f32[384,5120]{1,0:T(8,128)}), f32[384,1280]{1,0:T(8,128)}) %reduce-scatter.4.cloned.1.call-update) | async-done | bytes 1966096 | tf_op jit(solution)/shard_map/reduce_scatter | solution.py:63
  696.9 117.4 %all-reduce.6.cloned.1.call-done = (f32[4,64,1280]{2,1,0:T(8,128)}, f32[4,64,3584]{2,1,0:T(8,128)}) async-done(((f32[4,64,1280]{2,1,0:T(8,128)}, f32[4,64,3584]{2,1,0:T(8,128)}), (f32[4,64,1280]{2,1,0:T(8,128)}, f32[4,64,3584]{2,1,0:T(8,128)})) %all-reduce.6.cloned.1.call-update) | async-done | bytes 4980752 | tf_op jit(solution)/shard_map/psum | solution.py:79
  817.0 4.1 copy.29
  (58 shorter events, 32.7 us)
Async XLA Ops:
  7.2 149.0 %copy-start = (bf16[384,3584]{1,0:T(8,128)(2,1)S(1)}, bf16[384,3584]{1,0:T(8,128)(2,1)}, u32[]{:S(2)}) copy-start(bf16[384,3584]{1,0:T(8,128)(2,1)} %param.17) | copy-start | bytes 8257540
  31.7 88.4 %all-to-all-start.1 = ((bf16[4,2,229376]{2,1,0:T(2,128)(2,1)}), bf16[4,2,229376]{2,1,0:T(2,128)(2,1)}, u32[]{:S(2)}, u32[]{:S(2)}) async-start(bf16[4,2,229376]{2,1,0:T(2,128)(2,1)} %reshape.321), calls=%async_computation.1 | async-start | bytes 7340032 | tf_op jit(solution)/shard_map/all_to_all | solution.py:41
  120.2 38.6 %all-to-all-start = ((bf16[4,2,81920]{2,1,0:T(2,128)(2,1)}), bf16[4,2,81920]{2,1,0:T(2,128)(2,1)}, u32[]{:S(2)}, u32[]{:S(2)}) async-start(bf16[4,2,81920]{2,1,0:T(2,128)(2,1)} %reshape.323), calls=%async_computation | async-start | bytes 2621440 | tf_op jit(solution)/shard_map/all_to_all | solution.py:40
  124.5 79.6 %all-reduce.4.cloned.1.call-start = ((), (), s32[]{:S(2)}) async-start(), calls=%async_computation.8 | async-start | bytes 1572864 | tf_op jit(solution)/shard_map/psum | solution.py:58
  154.3 1.8 copy-start.2
  158.7 110.2 %all-gather.9.cloned.1.call-start = ((), (), s32[]{:S(2)}) async-start(), calls=%async_computation.11 | async-start | bytes 3932160 | tf_op jit(solution)/shard_map/all_gather | solution.py:47
  172.3 1.1 copy-start.3
  173.3 3.7 copy-start.7
  173.3 4.4 copy-start.6
  173.3 5.1 copy-start.9
  173.3 5.2 copy-start.8
  176.2 268.4 %all-gather.7.cloned.1.call-start = ((), (), s32[]{:S(2)}) async-start(), calls=%async_computation.6 | async-start | bytes 41287680 | tf_op jit(solution)/shard_map/all_gather | solution.py:38
  176.9 289.8 %reduce-scatter.6.cloned.1.call-start = ((), (), s32[]{:S(2)}) async-start(), calls=%async_computation.9 | async-start | bytes 3932160 | tf_op jit(solution)/shard_map/reduce_scatter | solution.py:76
  208.0 269.3 %reduce-scatter.8.cloned.1.call-start = ((), (), s32[]{:S(2)}) async-start(), calls=%async_computation.10 | async-start | bytes 11010048 | tf_op jit(solution)/shard_map/reduce_scatter | solution.py:77
  276.7 279.8 %all-gather.5.cloned.1.call-start = ((), (), s32[]{:S(2)}) async-start(), calls=%async_computation.5 | async-start | bytes 4915200 | tf_op jit(solution)/shard_map/all_gather | solution.py:37
  277.3 416.3 %reduce-scatter.4.cloned.1.call-start = ((), (), s32[]{:S(2)}) async-start(), calls=%async_computation.7 | async-start | bytes 9830400 | tf_op jit(solution)/shard_map/reduce_scatter | solution.py:63
  466.7 347.7 %all-reduce.6.cloned.1.call-start = ((), (), s32[]{:S(2)}) async-start(), calls=%async_computation.12 | async-start | bytes 9961472 | tf_op jit(solution)/shard_map/psum | solution.py:79
  580.4 113.2 %copy-start.4 = (bf16[4,2,64,1280]{3,2,1,0:T(8,128)(2,1)S(1)}, bf16[4,2,64,1280]{3,2,1,0:T(8,128)(2,1)}, u32[]{:S(2)}) copy-start(bf16[4,2,64,1280]{3,2,1,0:T(8,128)(2,1)} %copy-done.3) | copy-start | bytes 3932164
  580.4 113.2 %copy-start.5 = (f32[384,512]{1,0:T(8,128)S(1)}, f32[384,512]{1,0:T(8,128)}, u32[]{:S(2)}) copy-start(f32[384,512]{1,0:T(8,128)} %all-reduce.4.cloned.1.call-done) | copy-start | bytes 2359300
  814.3 6.8 copy-start.1
Sparse Core Ops, SparseCore 0:
  158.8 45.1 all-reduce.3
  206.2 62.6 all-gather.8
  270.8 173.7 all-gather.6
  447.2 10.4 reduce-scatter.5
  459.9 17.4 reduce-scatter.7
  478.8 77.6 all-gather.4
  558.8 134.7 reduce-scatter.3
  697.2 117.0 all-reduce.5
